TPU v7x, 256 devices: a whole 4x4x8 slice. The times are simulated.
256 devices in a mesh: rep: 16 (over z_hi, x), tp: 16 (over z_lo, y, core).
Axes of the slice: x: 4, y: 4, z: 8 (z_hi: 4, z_lo: 2; z = z_hi * 2 + z_lo), core: 2. Of those that a mesh axis runs over, the one named last changes fastest.
Arguments:
- tokens: bfloat16 [512, 4096], P(('rep', 'tp')), may hold values from -6 to 6
- conv_state: bfloat16 [3, 512, 8192], P(None, 'rep', 'tp'), may hold values from -6 to 6
- ssm_state: float32 [512, 16, 8192], P('rep', None, 'tp'), may hold values from -6 to 6
- norm_gains: bfloat16 [2, 4096], P(None, ('rep', 'tp')), may hold values from 0.5 to 1.5
- conv_weight: bfloat16 [4, 8192], P(None, ('rep', 'tp')), may hold values from -3 to 3
- conv_skip: bfloat16 [2, 8192], P(None, ('rep', 'tp')), may hold values from -3 to 3
- step_bias: bfloat16 [8192], P(('rep', 'tp')), may hold values from -5 to -1
- decay_log: bfloat16 [16, 8192], P(None, ('rep', 'tp')), may hold values from 0 to 2.796875
- input_proj: bfloat16 [4096, 2, 8192], P(('rep', 'tp')), may hold values from -0.09375 to 0.09375
- select_proj: bfloat16 [8192, 288], P('tp', 'rep'), may hold values from -0.0625 to 0.0625
- step_proj: bfloat16 [256, 8192], P(('rep', 'tp')), may hold values from -0.375 to 0.375
- output_proj: bfloat16 [8192, 4096], P(None, ('rep', 'tp')), may hold values from -0.0625 to 0.0625
- router: bfloat16 [4096, 16], P(('rep', 'tp')), may hold values from -0.09375 to 0.09375
- expert_proj: bfloat16 [4096, 2, 2, 12288], P(('rep', 'tp')), may hold values from -0.09375 to 0.09375
- expert_ids: int32 [512, 2], P(('rep', 'tp')), may hold values from 0 to 15, as said below
Outputs:
- mamba_out: bfloat16 [512, 4096], P(('rep', 'tp'))
- conv_next: bfloat16 [3, 512, 8192], P(None, 'rep', 'tp')
- ssm_next: float32 [512, 16, 8192], P('rep', None, 'tp')
- expert_hidden: bfloat16 [1024, 12288], P('rep', 'tp')
Inputs may be any that keep to these rules, and one draw needn't show every extreme that they name: `expert_ids`: each row names two different experts. Within each aligned block of 2 rows (the rows of one device) each expert e < 2 is named by at most 2 rows.
All inputs are finite; a program needn't handle non-finite values.
Results may differ from a plain program's by a relative error of at most 0.04.
Values may be sent and summed in bfloat16 or wider, within the bound.
A program may use at most 128 MiB of HBM per device.

v0:
```python
import math
import jax
import jax.numpy as jnp
from jax import lax
from jax.sharding import Mesh
from jax.sharding import PartitionSpec as P

CAPACITY = 2
REP_TP = ("rep_0", "rep_1", "tp")
REP = ("rep_0", "rep_1")
epsilon = 1e-05


def in_one_piece(arrays, axis, dim, along):
    widths = [a.shape[along] for a in arrays]
    both = jnp.concatenate(arrays, axis=along)
    out = lax.all_gather(both, axis, axis=dim, tiled=True)
    return tuple(jnp.split(out, [sum(widths[:k]) for k in range(1, len(widths))], axis=along))


def from_everyone(array, axis):
    devices = lax.axis_size(axis)
    return lax.all_to_all(
        jnp.broadcast_to(array[None], (devices, *array.shape)), axis, 0, 0, tiled=True
    )


def joined_along(blocks, dim):
    dims = list(blocks.shape[1:])
    dims[dim] *= blocks.shape[0]
    return jnp.moveaxis(blocks, 0, dim).reshape(dims)


def gathered_copies(array, axis, dim):
    blocks = from_everyone(array, axis)
    return joined_along(blocks, dim)


def gather_packed(arrays, axis, dims):
    ravelled = jnp.concatenate([a.reshape(-1) for a in arrays])
    lines, at, outs = (lax.all_gather(ravelled, axis), 0, [])
    for a, dim in zip(arrays, dims):
        blocks = lines[:, at : at + a.size].reshape(-1, *a.shape)
        outs.append(joined_along(blocks, dim))
        at += a.size
    return tuple(outs)


def over_copies(array, axis):
    return from_everyone(array, axis).astype(jnp.float32).sum(axis=0)


def split_up(array, dim, devices):
    before, after = (array.shape[:dim], array.shape[dim + 1 :])
    return jnp.moveaxis(array.reshape(*before, devices, -1, *after), dim, 0)


def sent_and_summed(array, axis, dim):
    devices = lax.axis_size(axis)
    blocks = lax.all_to_all(split_up(array, dim, devices), axis, 0, 0, tiled=True)
    return jnp.sum(blocks.astype(jnp.float32), axis=0)


def side_by_side(arrays, axis, dim, along):
    widths = [math.prod(a.shape[along:]) for a in arrays]
    both = jnp.concatenate(
        [a.reshape(*a.shape[:along], w) for a, w in zip(arrays, widths)], axis=along
    )
    out = lax.all_gather(both, axis, axis=dim, tiled=True)
    blocks = jnp.split(out, [sum(widths[:k]) for k in range(1, len(widths))], axis=along)
    return tuple((b.reshape(*out.shape[:along], *a.shape[along:]) for a, b in zip(arrays, blocks)))


def own_block(blocks, axes, order):
    dims = [lax.axis_size(a) for a in axes]
    blocks = blocks.reshape(*dims, *blocks.shape[1:])
    blocks = blocks.transpose(*order, *range(len(axes), blocks.ndim))
    blocks = blocks.reshape(-1, *blocks.shape[len(axes) :])
    for k in order:
        blocks = lax.psum_scatter(blocks, axes[k], scatter_dimension=0, tiled=True)
    return blocks[0]


def scatter_axes(array, axes, order, dim):
    devices = lax.axis_size(axes)
    return own_block(split_up(array, dim, devices), axes, order)


def norm_scale(values, gain):
    mean_square = jnp.mean(values * values, axis=-1, keepdims=True)
    return values * lax.rsqrt(mean_square + epsilon) * gain.astype(jnp.float32)


def shards(
    tokens,
    conv_state,
    ssm_state,
    norm_gains,
    conv_weight,
    conv_skip,
    step_bias,
    decay_log,
    input_proj,
    select_proj,
    step_proj,
    output_proj,
    router,
    expert_proj,
    expert_ids,
):
    tp_count = lax.axis_size("tp")
    tp_index = lax.axis_index("tp")
    norm_gain, conv_taps, skip_rows, shift_full, decay_full, router_full = (
        lax.all_gather(norm_gains, REP_TP, axis=1, tiled=True),
        *in_one_piece((conv_weight, conv_skip), REP_TP, 1, 0),
        lax.all_gather(step_bias, REP_TP, axis=0, tiled=True),
        lax.all_gather(decay_log, REP_TP, axis=1, tiled=True),
        lax.all_gather(router, REP_TP, axis=0, tiled=True),
    )
    inner_dev = ssm_state.shape[2]
    channel_start = tp_index * inner_dev
    conv_taps = lax.dynamic_slice_in_dim(conv_taps, channel_start, inner_dev, 1).astype(jnp.float32)
    skip_rows = lax.dynamic_slice_in_dim(skip_rows, channel_start, inner_dev, 1).astype(jnp.float32)
    shift_dev = lax.dynamic_slice_in_dim(shift_full, channel_start, inner_dev, 0).astype(
        jnp.float32
    )
    decay_dev = lax.dynamic_slice_in_dim(decay_full, channel_start, inner_dev, 1).astype(
        jnp.float32
    )
    model_rows = input_proj.shape[0]
    inner_all = input_proj.shape[2]
    input_blocks, expert_blocks, step_blocks = (
        lax.all_to_all(
            input_proj.reshape(model_rows, 1, 2, inner_all),
            "tp",
            split_axis=3,
            concat_axis=0,
            tiled=True,
        ),
        lax.all_to_all(expert_proj, "tp", split_axis=3, concat_axis=0, tiled=True),
        lax.all_to_all(
            step_proj.reshape(step_proj.shape[0], 1, 1, inner_all),
            "tp",
            split_axis=3,
            concat_axis=0,
            tiled=True,
        ),
    )
    output_blocks = lax.all_to_all(output_proj, "tp", split_axis=0, concat_axis=1, tiled=True)
    residual_in = tokens.astype(jnp.float32)
    normed = norm_scale(residual_in, norm_gain[0]).astype(jnp.bfloat16)
    features = gathered_copies(normed, "tp", 0)
    shard_piece = lax.all_gather(input_blocks, REP, axis=0, tiled=True)
    piece_rows = shard_piece.shape[0]
    projected = jnp.dot(
        features, shard_piece.reshape(piece_rows, 2 * inner_dev), preferred_element_type=jnp.float32
    )
    output_rows, step_rows, select_rows = gather_packed(
        (output_blocks, step_blocks, select_proj), REP, (1, 0, 1)
    )
    step_rows = step_rows.reshape(step_rows.shape[0], inner_dev)
    step_rank = step_rows.shape[0]
    state_count = ssm_state.shape[1]
    conv_input = projected[:, :inner_dev]
    gate_z = projected[:, inner_dev:]
    history = conv_state.astype(jnp.float32)
    conv_mix = (
        jnp.sum(conv_taps[:-1, None, :] * history, axis=0)
        + conv_taps[-1] * conv_input
        + skip_rows[0]
    )
    conv_next = jnp.concatenate([conv_state[1:], conv_input.astype(jnp.bfloat16)[None]], axis=0)
    activated = jax.nn.silu(conv_mix)
    select_part = jnp.dot(
        activated.astype(jnp.bfloat16), select_rows, preferred_element_type=jnp.float32
    )
    selected = over_copies(select_part.astype(jnp.bfloat16), "tp").astype(jnp.float32)
    step_low = selected[:, :step_rank].astype(jnp.bfloat16)
    input_map = selected[:, step_rank : step_rank + state_count]
    output_map = selected[:, step_rank + state_count :]
    step_size = jax.nn.softplus(
        jnp.dot(step_low, step_rows, preferred_element_type=jnp.float32) + shift_dev
    )
    decay_rate = -jnp.exp(decay_dev)
    factor = jnp.exp(step_size[:, None, :] * decay_rate[None])
    ssm_next = factor * ssm_state + (step_size * activated)[:, None, :] * input_map[:, :, None]
    readout = jnp.sum(ssm_next * output_map[:, :, None], axis=1) + skip_rows[1] * activated
    gated_out = (readout * jax.nn.silu(gate_z)).astype(jnp.bfloat16)
    output_part = jnp.dot(gated_out, output_rows, preferred_element_type=jnp.float32)
    mixer_out = sent_and_summed(output_part.astype(jnp.bfloat16), "tp", 0)
    residual = residual_in + mixer_out
    mamba_out = residual.astype(jnp.bfloat16)
    moe_in = norm_scale(residual, norm_gain[1]).astype(jnp.bfloat16)
    logits = jnp.dot(moe_in, router_full, preferred_element_type=jnp.float32)
    expert_total = logits.shape[1]
    choose = (
        expert_ids[:, :, None] == jnp.arange(expert_total, dtype=jnp.int32)[None, None, :]
    ).astype(jnp.float32)
    picked = jnp.sum(choose * logits[:, None, :], axis=2)
    first_gate = jax.nn.sigmoid(picked[:, 0] - picked[:, 1])
    second_gate = jax.nn.sigmoid(picked[:, 1] - picked[:, 0])
    window_count = expert_blocks.shape[1]
    window = jnp.arange(window_count, dtype=jnp.int32)
    names_first = expert_ids[:, 0:1] == window[None, :]
    names_second = expert_ids[:, 1:2] == window[None, :]
    zero = jnp.zeros((), jnp.float32)
    gate_w = jnp.where(names_first, first_gate[:, None], zero) + jnp.where(
        names_second, second_gate[:, None], zero
    )
    routed = (names_first | names_second).astype(jnp.int32)
    position = jnp.cumsum(routed, axis=0) - routed
    slot_of = (position[:, :, None] == jnp.arange(CAPACITY, dtype=jnp.int32)[None, None, :]) & (
        routed[:, :, None] > 0
    )
    slot_x = jnp.einsum(
        "tec,td->ecd", slot_of.astype(jnp.bfloat16), moe_in, preferred_element_type=jnp.float32
    )
    slot_local = window_count * CAPACITY
    slot_x = slot_x.astype(jnp.bfloat16).reshape(slot_local, moe_in.shape[1])
    slot_gate = (
        jnp.einsum("tec,te->ec", slot_of.astype(jnp.float32), gate_w)
        .astype(jnp.bfloat16)
        .reshape(slot_local)
    )
    feature_rows = expert_blocks.shape[0]
    replica_rows, gate_all = side_by_side((slot_x, slot_gate), "tp", 0, 1)
    gathered = lax.all_to_all(replica_rows, REP, split_axis=1, concat_axis=0, tiled=True)
    hidden_dev = expert_blocks.shape[3]
    group_rows = tp_count * slot_local
    picked_rows = gathered
    picked_rows = picked_rows.reshape(
        group_rows * lax.axis_size(REP) // slot_local, window_count, CAPACITY, feature_rows
    )
    product = jnp.einsum(
        "gecd,dexf->gecxf", picked_rows, expert_blocks, preferred_element_type=jnp.float32
    )
    summed = scatter_axes(
        product.reshape(group_rows * lax.axis_size(REP), 2 * hidden_dev).astype(jnp.bfloat16),
        REP,
        (1, 0),
        0,
    ).astype(jnp.float32)
    hidden = (
        gate_all.astype(jnp.float32)[:, None]
        * jax.nn.silu(summed[:, :hidden_dev])
        * summed[:, hidden_dev:]
    )
    expert_hidden = hidden.astype(jnp.bfloat16)
    return (mamba_out, conv_next, ssm_next, expert_hidden)


def solution(mesh):
    split = Mesh(mesh.devices.reshape(4, 4, mesh.shape["tp"]), ("rep_0", "rep_1", "tp"))
    return jax.shard_map(
        shards,
        mesh=split,
        in_specs=(
            P(REP_TP, None),
            P(None, REP, "tp"),
            P(REP, None, "tp"),
            P(None, REP_TP),
            P(None, REP_TP),
            P(None, REP_TP),
            P(REP_TP),
            P(None, REP_TP),
            P(REP_TP, None, None),
            P("tp", REP),
            P(REP_TP, None),
            P(None, REP_TP),
            P(REP_TP, None),
            P(REP_TP, None, None, None),
            P(REP_TP, None),
        ),
        out_specs=(P(REP_TP, None), P(None, REP, "tp"), P(REP, None, "tp"), P(REP, "tp")),
        check_vma=False,
    )
```

profile of v0, /device:TPU:2, one launch (start us, length us, event | category | flops | bytes accessed | tf_op | source)
XLA Modules:
  0.0 1973.0 jit_solution(4106802272947335639)
XLA Ops:
  7.2 8.3 copy.135
  16.0 62.6 %reduce.12 = bf16[8192]{0:T(1024)(128)(2,1)S(1)} reduce(bf16[8192,1,1,1]{3,2,1,0:T(2,128)(2,1)} %bitcast.104, bf16[]{:T(256)} %broadcast.160), dimensions={1,2,3}, to_apply=%bitcast.77.reduce_sub_computation | reduce | bytes 32770
  95.0 8.4 reshape.274
  103.4 62.0 %bitcast_reduce_fusion = bf16[8192]{0:T(1024)(128)(2,1)S(1)} fusion(bf16[8192,1,1,1]{3,2,1,0:T(2,128)(2,1)} %reshape.274), kind=kLoop, calls=%fused_computation.72 | loop fusion | bytes 32768 | tf_op jit(solution)/shard_map/all_to_all | solution.py:141
  169.6 6.8 copy.129
  176.3 7.7 bitcast_bitcast_fusion
  189.8 18.9 all_to_all.92
  212.8 10.3 copy.152
  223.2 333.4 %all-gather.2 = bf16[256,16,2]{1,2,0:T(2,128)(2,1)S(1)} all-gather(bf16[1,16,2]{1,2,0:T(2,128)(2,1)S(1)} %bitcast.128), channel_id=1, replica_groups=mesh['rep_0'=4,'rep_1'=4,'tp'=16] {'rep_0','rep_1','tp'}, dimensions={0}, use_global_device_ids=true | all-gather | bytes 16448 | tf_op jit(solution)/shard_map/all_gather | solution.py:114
  561.5 342.0 %all-gather.1 = bf16[256,32,6]{1,2,0:T(8,128)(2,1)S(1)} all-gather(bf16[1,32,6]{1,2,0:T(8,128)(2,1)S(1)} %maximum_bitcast_fusion.1), channel_id=1, replica_groups=mesh['rep_0'=4,'rep_1'=4,'tp'=16] {'rep_0','rep_1','tp'}, dimensions={0}, use_global_device_ids=true | all-gather | bytes 98688 | tf_op jit(solution)/shard_map/all_gather | solution.py:17
  916.6 11.3 copy.132
  927.9 6.0 fusion.24
  938.5 344.1 %all-gather.3 = bf16[256,32,16]{1,2,0:T(8,128)(2,1)S(1)} all-gather(bf16[1,32,16]{1,2,0:T(8,128)(2,1)S(1)} %bitcast.126), channel_id=1, replica_groups=mesh['rep_0'=4,'rep_1'=4,'tp'=16] {'rep_0','rep_1','tp'}, dimensions={0}, use_global_device_ids=true | all-gather | bytes 263168 | tf_op jit(solution)/shard_map/all_gather | solution.py:117
  1284.3 98.4 %all-reduce = bf16[8192]{0:T(1024)(128)(2,1)S(1)} all-reduce(bf16[8192]{0:T(1024)(128)(2,1)S(1)} %dynamic-update-slice), channel_id=1, replica_groups=mesh['rep_0'=4,'rep_1'=4,'tp'=16] {'rep_0','rep_1','tp'}, use_global_device_ids=true, to_apply=%add | all-reduce | flops 8192 | bytes 32768
  1392.6 6.5 copy.139
  1410.8 20.2 %copy.142 = bf16[16,2,2,12288]{0,2,1,3:T(2,128)(2,1)} copy(bf16[16,2,2,12288]{3,2,1,0:T(2,128)(2,1)S(1)} %copy-done.1) | data formatting | bytes 3145728 | tf_op args[13]
  1430.9 17.7 reshape.277
  1448.6 328.0 %all_gather.34 = bf16[4096,16]{1,0:T(8,128)(2,1)S(1)} all-gather(bf16[16,16]{1,0:T(8,128)(2,1)S(1)} %copy-done.10), channel_id=1, replica_groups=mesh['rep_0'=4,'rep_1'=4,'tp'=16] {'rep_0','rep_1','tp'}, dimensions={0}, use_global_device_ids=true | all-gather | bytes 131584 | tf_op jit(solution)/shard_map/all_gather | solution.py:118
  1782.5 32.2 %all-gather.4 = bf16[16,4,4097]{2,1,0:T(4,128)(2,1)S(1)} all-gather(bf16[1,4,4097]{2,1,0:T(4,128)(2,1)S(1)} %maximum_bitcast_fusion), channel_id=1, replica_groups=mesh['rep_0'=4,'rep_1'=4,'tp'=16] {'tp'}, dimensions={0}, use_global_device_ids=true | all-gather | bytes 557192 | tf_op jit(solution)/shard_map/all_gather | solution.py:69
  1816.0 25.0 %all-to-all-start.6 = ((bf16[64,16,256]{2,0,1:T(8,128)(2,1)}), bf16[64,16,256]{2,0,1:T(8,128)(2,1)S(1)}, u32[]{:S(2)}, u32[]{:S(2)}) async-start(bf16[64,16,256]{2,0,1:T(8,128)(2,1)} %bitcast.95), calls=%async_computation.6 | async-start | bytes 1048576 | tf_op jit(solution)/shard_map/all_to_all | solution.py:227
  1841.1 12.1 reshape.278
  1853.2 26.5 %copy.143 = bf16[16,2,2,16,768]{4,0,3,2,1:T(8,128)(2,1)S(1)} copy(bf16[16,2,2,16,768]{0,2,1,4,3:T(2,128)(2,1)} %bitcast.98) | data formatting | bytes 3145728 | tf_op jit(solution)/shard_map/all_to_all | solution.py:140
  1891.5 39.0 %reduce-scatter.3.cloned.1.call-done = bf16[4,64,1536]{2,1,0:T(8,128)(2,1)} async-done(((bf16[16,64,1536]{2,1,0:T(8,128)(2,1)}), bf16[4,64,1536]{2,1,0:T(8,128)(2,1)}) %reduce-scatter.3.cloned.1.call-update) | async-done | bytes 786448 | tf_op jit(solution)/shard_map/reduce_scatter | solution.py:80
  1932.0 32.7 %reduce-scatter.5.cloned.1.call-done = bf16[1,64,1536]{2,1,0:T(8,128)(2,1)} async-done(((bf16[4,64,1536]{2,1,0:T(8,128)(2,1)}), bf16[1,64,1536]{2,1,0:T(8,128)(2,1)}) %reduce-scatter.5.cloned.1.call-update) | async-done | bytes 196624 | tf_op jit(solution)/shard_map/reduce_scatter | solution.py:80
  (139 shorter events, 98.6 us)
Async XLA Ops:
  7.2 78.0 %copy-start.6 = (bf16[8192,16]{0,1:T(8,128)(2,1)S(1)}, bf16[8192,16]{0,1:T(8,128)(2,1)}, u32[]{:S(2)}) copy-start(bf16[8192,16]{0,1:T(8,128)(2,1)} %param.26) | copy-start | bytes 786436
  7.2 78.7 %copy-start.7 = (bf16[512,18]{0,1:T(8,128)(2,1)S(1)}, bf16[512,18]{0,1:T(8,128)(2,1)}, u32[]{:S(2)}) copy-start(bf16[512,18]{0,1:T(8,128)(2,1)} %param.24) | copy-start | bytes 55300
  79.2 12.0 all-to-all-start.3
  91.2 74.2 %all-to-all-start.2 = ((bf16[16,512,16]{1,2,0:T(8,128)(2,1)}), bf16[16,512,16]{1,2,0:T(8,128)(2,1)S(1)}, u32[]{:S(2)}, u32[]{:S(2)}) async-start(bf16[16,512,16]{1,2,0:T(8,128)(2,1)} %bitcast.96), calls=%async_computation.2 | async-start | bytes 524288 | tf_op jit(solution)/shard_map/all_to_all | solution.py:149
  94.8 809.6 %all-gather.10.cloned.1.call-start = ((), (), s32[]{:S(2)}) async-start(), calls=%async_computation.13 | async-start | bytes 5048320 | tf_op jit(solution)/shard_map/all_gather | solution.py:41
  103.4 66.2 %copy-start.3 = (bf16[16,2,8192]{2,1,0:T(2,128)(2,1)S(1)}, bf16[16,2,8192]{2,1,0:T(2,128)(2,1)}, u32[]{:S(2)}) copy-start(bf16[16,2,8192]{2,1,0:T(2,128)(2,1)} %param.23) | copy-start | bytes 1572868
  169.5 747.1 %all-gather.8.cloned.1.call-start = ((), (), s32[]{:S(2)}) async-start(), calls=%async_computation.10 | async-start | bytes 8912896 | tf_op jit(solution)/shard_map/all_gather | solution.py:153
  208.7 14.5 copy-start.12
  208.7 348.1 %copy-start.5 = (bf16[2,4096]{1,0:T(2,128)(2,1)S(1)}, bf16[2,4096]{1,0:T(2,128)(2,1)}, u32[]{:S(2)}) copy-start(bf16[2,4096]{1,0:T(2,128)(2,1)} %param.15) | copy-start | bytes 49156
  212.8 348.7 %copy-start.11 = (bf16[4,32]{1,0:T(4,128)(2,1)S(1)}, bf16[4,32]{1,0:T(4,128)(2,1)}, u32[]{:S(2)}) copy-start(bf16[4,32]{1,0:T(4,128)(2,1)} %param.19) | copy-start | bytes 772
  212.8 348.7 %copy-start.13 = (bf16[2,32]{1,0:T(2,128)(2,1)S(1)}, bf16[2,32]{1,0:T(2,128)(2,1)}, u32[]{:S(2)}) copy-start(bf16[2,32]{1,0:T(2,128)(2,1)} %param.20) | copy-start | bytes 388
  212.8 691.3 %copy-start.4 = (bf16[3,32,512]{2,1,0:T(8,128)(2,1)S(1)}, bf16[3,32,512]{2,1,0:T(8,128)(2,1)}, u32[]{:S(2)}) copy-start(bf16[3,32,512]{2,1,0:T(8,128)(2,1)} %param.16) | copy-start | bytes 294916
  558.0 346.2 %all-to-all-start = ((bf16[16,2,4096]{2,1,0:T(2,128)(2,1)}), bf16[16,2,4096]{2,1,0:T(2,128)(2,1)S(1)}, u32[]{:S(2)}, u32[]{:S(2)}) async-start(bf16[16,2,4096]{2,1,0:T(2,128)(2,1)} %broadcast_in_dim.24), calls=%async_computation | async-start | bytes 524288 | tf_op jit(solution)/shard_map/all_to_all | solution.py:23
  933.9 350.1 %copy-start.14 = (bf16[32]{0:T(256)(128)(2,1)S(1)}, bf16[32]{0:T(256)(128)(2,1)}, u32[]{:S(2)}) copy-start(bf16[32]{0:T(256)(128)(2,1)} %param.21) | copy-start | bytes 196
  933.9 448.8 %copy-start.8 = (s32[2,2]{1,0:T(2,128)S(1)}, s32[2,2]{1,0:T(2,128)}, u32[]{:S(2)}) copy-start(s32[2,2]{1,0:T(2,128)} %param.29) | copy-start | bytes 52
  934.9 464.2 %all-to-all-start.4 = ((bf16[16,32,288]{2,1,0:T(8,128)(2,1)}), bf16[16,32,288]{2,1,0:T(8,128)(2,1)S(1)}, u32[]{:S(2)}, u32[]{:S(2)}) async-start(bf16[16,32,288]{2,1,0:T(8,128)(2,1)} %broadcast_in_dim.25), calls=%async_computation.4 | async-start | bytes 786432 | tf_op jit(solution)/shard_map/all_to_all | solution.py:23
  1405.3 371.3 %all-to-all-start.5 = ((bf16[16,2,4096]{2,1,0:T(2,128)(2,1)}), bf16[16,2,4096]{2,1,0:T(2,128)(2,1)S(1)}, u32[]{:S(2)}, u32[]{:S(2)}) async-start(bf16[16,2,4096]{2,1,0:T(2,128)(2,1)} %reshape.243), calls=%async_computation.5 | async-start | bytes 524288 | tf_op jit(solution)/shard_map/all_to_all | solution.py:60
  1430.9 17.7 copy-start.10
  1776.6 39.4 %all-to-all-start.7 = ((bf16[16,2,24576]{2,1,0:T(2,128)(2,1)}), bf16[16,2,24576]{2,1,0:T(2,128)(2,1)S(1)}, u32[]{:S(2)}, u32[]{:S(2)}) async-start(bf16[16,2,24576]{2,1,0:T(2,128)(2,1)} %reshape.277), calls=%async_computation.7 | async-start | bytes 3145728 | tf_op jit(solution)/shard_map/all_to_all | solution.py:140
  1815.0 38.2 %copy-start = (bf16[64,4097]{1,0:T(8,128)(2,1)}, bf16[64,4097]{1,0:T(8,128)(2,1)S(1)}, u32[]{:S(2)}) copy-start(bf16[64,4097]{1,0:T(8,128)(2,1)S(1)} %reshape.261) | copy-start | bytes 1573252
  1816.0 63.7 %all-to-all-start.6 = ((bf16[64,16,256]{2,0,1:T(8,128)(2,1)}), bf16[64,16,256]{2,0,1:T(8,128)(2,1)S(1)}, u32[]{:S(2)}, u32[]{:S(2)}) async-start(bf16[64,16,256]{2,0,1:T(8,128)(2,1)} %bitcast.95), calls=%async_computation.6 | async-start | bytes 1048576 | tf_op jit(solution)/shard_map/all_to_all | solution.py:227
  1841.0 89.4 %reduce-scatter.3.cloned.1.call-start = ((), (), s32[]{:S(2)}) async-start(), calls=%async_computation.11 | async-start | bytes 3932160 | tf_op jit(solution)/shard_map/reduce_scatter | solution.py:80
  1887.5 43.0 %slice-start.1 = ((bf16[3,32,512]{2,1,0:T(8,128)(2,1)}), bf16[2,32,512]{2,1,0:T(8,128)(2,1)S(1)}, s32[]{:S(2)}) async-start(bf16[3,32,512]{2,1,0:T(8,128)(2,1)} %param.16), calls=%async_computation.15 | async-start | bytes 131072 | tf_op jit(solution)/shard_map/slice | solution.py:172
  1891.4 73.2 %reduce-scatter.5.cloned.1.call-start = ((), (), s32[]{:S(2)}) async-start(), calls=%async_computation.12 | async-start | bytes 983040 | tf_op jit(solution)/shard_map/reduce_scatter | solution.py:80
  (4 other events, 33.4 us)
Sparse Core Ops, SparseCore 0:
  169.6 81.2 all-gather.9
  253.9 117.8 all-gather.7
  1891.5 38.8 reduce-scatter.2
  1932.9 31.7 reduce-scatter.4
where the time goes:
time: 1980 us; the launch traced here: 1970 us
  blocking collectives  1500 us (76%)
  local copies, waits for them, and re-layouts  252 us (13%)
  waiting for transfers between devices  76.8 us (4%)
  other arithmetic  70.1 us (4%)
  starting transfers between devices  51.1 us (3%)
    all_gather x1, blocking collectives, shards(): lax.all_gather(decay_log, REP_TP, axis=1, tiled=True)  344 us
    all_gather x1, blocking collectives, in_one_piece(): out = lax.all_gather(both, axis, axis=dim, tiled=True)  342 us
    all_gather x1, blocking collectives, shards(): lax.all_gather(norm_gains, REP_TP, axis=1, tiled=True)  333 us
    all_gather x1, blocking collectives, shards(): lax.all_gather(router, REP_TP, axis=0, tiled=True)  328 us
    unnamed x1, blocking collectives  98.4 us
    unnamed x48, local copies, waits for them, and re-layouts  91.4 us
    reduce_scatter x2, waiting for transfers between devices, own_block(): blocks = lax.psum_scatter(blocks, axes[k], scatter_dimension=0, tiled=True)  71.6 us
    unnamed x3, other arithmetic  62.6 us
  transfers between devices with their start and end apart: 11, of which 3 were waited for; matrix products, arithmetic and copies ran while one was open for 11% of the time, Pallas kernels for 0%

commit v1 on v0

--- a/solution.py
+++ b/solution.py
@@ -9,6 +9,11 @@
 REP_TP = ("rep_0", "rep_1", "tp")
 REP = ("rep_0", "rep_1")
 epsilon = 1e-05
+
+
+def swapped_in(x, name, dim):
+    repeated = jnp.stack([x] * lax.axis_size(name))
+    return jnp.concatenate(lax.all_to_all(repeated, name, 0, 0), axis=dim)
 
 
 def in_one_piece(arrays, axis, dim, along):
@@ -111,7 +116,7 @@
     tp_count = lax.axis_size("tp")
     tp_index = lax.axis_index("tp")
     norm_gain, conv_taps, skip_rows, shift_full, decay_full, router_full = (
-        lax.all_gather(norm_gains, REP_TP, axis=1, tiled=True),
+        swapped_in(norm_gains, REP_TP, 1),
         *in_one_piece((conv_weight, conv_skip), REP_TP, 1, 0),
         lax.all_gather(step_bias, REP_TP, axis=0, tiled=True),
         lax.all_gather(decay_log, REP_TP, axis=1, tiled=True),

time: 1980 us -> 1660 us (0.84)
  blocking collectives: 1500 us -> 1160 us
    all_gather x1 -> x0, blocking collectives: 333 us -> none  [shards(): lax.all_gather(norm_gains, REP_TP, axis=1, tiled=True)]
    unnamed x48 -> x47, local copies, waits for them, and re-layouts: 91.4 us -> 91.3 us
  transfers between devices with their start and end apart: 11 -> 12, of which waited for: 3 -> 4; matrix products, arithmetic and copies ran while one was open for 11% -> 13% of each run, Pallas kernels for 0% -> 0%
where the time goes in v1:
time: 1660 us; the launch traced here: 1650 us
  blocking collectives  1160 us (70%)
  local copies, waits for them, and re-layouts  254 us (15%)
  waiting for transfers between devices  84.6 us (5%)
  other arithmetic  70.8 us (4%)
  starting transfers between devices  60 us (4%)
    all_gather x1, blocking collectives, shards(): lax.all_gather(decay_log, REP_TP, axis=1, tiled=True)  344 us
    all_gather x1, blocking collectives, in_one_piece(): out = lax.all_gather(both, axis, axis=dim, tiled=True)  337 us
    all_gather x1, blocking collectives, shards(): lax.all_gather(router, REP_TP, axis=0, tiled=True)  328 us
    unnamed x1, blocking collectives  99.5 us
    unnamed x47, local copies, waits for them, and re-layouts  91.3 us
    reduce_scatter x2, waiting for transfers between devices, own_block(): blocks = lax.psum_scatter(blocks, axes[k], scatter_dimension=0, tiled=True)  71.7 us
    unnamed x3, other arithmetic  62.6 us
    all_to_all x1, local copies, waits for them, and re-layouts, shards(): lax.all_to_all(step_proj.reshape(step_proj.shape[0], 1, 1, inner_all), 't...  62 us
  transfers between devices with their start and end apart: 12, of which 4 were waited for; matrix products, arithmetic and copies ran while one was open for 13% of the time, Pallas kernels for 0%

profile of v1, /device:TPU:2, one launch (start us, length us, event | category | flops | bytes accessed | tf_op | source)
XLA Modules:
  0.0 1653.9 jit_solution(902156170161684680)
XLA Ops:
  7.2 8.3 copy.128
  16.0 62.6 %reduce.20 = bf16[8192]{0:T(1024)(128)(2,1)S(1)} reduce(bf16[8192,1,1,1]{3,2,1,0:T(2,128)(2,1)} %bitcast.97, bf16[]{:T(256)} %broadcast.168), dimensions={1,2,3}, to_apply=%bitcast.70.reduce_sub_computation | reduce | bytes 32770
  95.0 8.4 reshape.309
  103.4 62.0 %bitcast_reduce_fusion = bf16[8192]{0:T(1024)(128)(2,1)S(1)} fusion(bf16[8192,1,1,1]{3,2,1,0:T(2,128)(2,1)} %reshape.309), kind=kLoop, calls=%fused_computation.74 | loop fusion | bytes 32768 | tf_op jit(solution)/shard_map/all_to_all | solution.py:146
  169.6 6.8 copy.122
  176.3 7.7 bitcast_bitcast_fusion
  189.8 18.9 %all_to_all.97 = bf16[16,2,8192]{2,1,0:T(2,128)(2,1)S(1)} all-to-all(bf16[16,2,8192]{2,1,0:T(2,128)(2,1)S(1)} %reshape.310), channel_id=1, replica_groups=mesh['rep_0'=4,'rep_1'=4,'tp'=16] {'tp'}, dimensions={0} | all-to-all | bytes 1048576 | tf_op jit(solution)/shard_map/all_to_all | solution.py:138
  212.8 10.3 copy.145
  223.9 8.9 all-to-all-start
  233.0 336.7 %all-gather.1 = bf16[256,32,6]{1,2,0:T(8,128)(2,1)S(1)} all-gather(bf16[1,32,6]{1,2,0:T(8,128)(2,1)S(1)} %maximum_bitcast_fusion.1), channel_id=1, replica_groups=mesh['rep_0'=4,'rep_1'=4,'tp'=16] {'rep_0','rep_1','tp'}, dimensions={0}, use_global_device_ids=true | all-gather | bytes 98688 | tf_op jit(solution)/shard_map/all_gather | solution.py:22
  575.9 7.8 all-to-all-done.1
  596.1 11.7 copy.125
  618.4 343.8 %all-gather.2 = bf16[256,32,16]{1,2,0:T(8,128)(2,1)S(1)} all-gather(bf16[1,32,16]{1,2,0:T(8,128)(2,1)S(1)} %bitcast.117), channel_id=1, replica_groups=mesh['rep_0'=4,'rep_1'=4,'tp'=16] {'rep_0','rep_1','tp'}, dimensions={0}, use_global_device_ids=true | all-gather | bytes 263168 | tf_op jit(solution)/shard_map/all_gather | solution.py:122
  963.9 99.5 %all-reduce = bf16[8192]{0:T(1024)(128)(2,1)S(1)} all-reduce(bf16[8192]{0:T(1024)(128)(2,1)S(1)} %dynamic-update-slice), channel_id=1, replica_groups=mesh['rep_0'=4,'rep_1'=4,'tp'=16] {'rep_0','rep_1','tp'}, use_global_device_ids=true, to_apply=%add | all-reduce | flops 8192 | bytes 32768
  1073.3 6.5 copy.132
  1091.5 20.2 %copy.135 = bf16[16,2,2,12288]{0,2,1,3:T(2,128)(2,1)} copy(bf16[16,2,2,12288]{3,2,1,0:T(2,128)(2,1)S(1)} %copy-done.1) | data formatting | bytes 3145728 | tf_op args[13]
  1111.7 17.7 %reshape.312 = bf16[16,2,24576]{2,1,0:T(2,128)(2,1)} reshape(bf16[12288,2,2,16]{3,2,1,0:T(2,128)(2,1)} %bitcast.92) | data formatting | bytes 3145728
  1129.3 328.0 %all_gather.30 = bf16[4096,16]{1,0:T(8,128)(2,1)S(1)} all-gather(bf16[16,16]{1,0:T(8,128)(2,1)S(1)} %copy-done.10), channel_id=1, replica_groups=mesh['rep_0'=4,'rep_1'=4,'tp'=16] {'rep_0','rep_1','tp'}, dimensions={0}, use_global_device_ids=true | all-gather | bytes 131584 | tf_op jit(solution)/shard_map/all_gather | solution.py:123
  1463.4 32.2 %all-gather.3 = bf16[16,4,4097]{2,1,0:T(4,128)(2,1)S(1)} all-gather(bf16[1,4,4097]{2,1,0:T(4,128)(2,1)S(1)} %maximum_bitcast_fusion), channel_id=1, replica_groups=mesh['rep_0'=4,'rep_1'=4,'tp'=16] {'tp'}, dimensions={0}, use_global_device_ids=true | all-gather | bytes 557192 | tf_op jit(solution)/shard_map/all_gather | solution.py:74
  1496.9 25.0 %all-to-all-start.7 = ((bf16[64,16,256]{2,0,1:T(8,128)(2,1)}), bf16[64,16,256]{2,0,1:T(8,128)(2,1)S(1)}, u32[]{:S(2)}, u32[]{:S(2)}) async-start(bf16[64,16,256]{2,0,1:T(8,128)(2,1)} %bitcast.88), calls=%async_computation.7 | async-start | bytes 1048576 | tf_op jit(solution)/shard_map/all_to_all | solution.py:232
  1521.9 12.1 reshape.313
  1534.1 26.5 %copy.136 = bf16[16,2,2,16,768]{4,0,3,2,1:T(8,128)(2,1)S(1)} copy(bf16[16,2,2,16,768]{0,2,1,4,3:T(2,128)(2,1)} %bitcast.91) | data formatting | bytes 3145728 | tf_op jit(solution)/shard_map/all_to_all | solution.py:145
  1572.3 39.0 %reduce-scatter.3.cloned.1.call-done = bf16[4,64,1536]{2,1,0:T(8,128)(2,1)} async-done(((bf16[16,64,1536]{2,1,0:T(8,128)(2,1)}), bf16[4,64,1536]{2,1,0:T(8,128)(2,1)}) %reduce-scatter.3.cloned.1.call-update) | async-done | bytes 786448 | tf_op jit(solution)/shard_map/reduce_scatter | solution.py:85
  1612.8 32.7 %reduce-scatter.5.cloned.1.call-done = bf16[1,64,1536]{2,1,0:T(8,128)(2,1)} async-done(((bf16[4,64,1536]{2,1,0:T(8,128)(2,1)}), bf16[1,64,1536]{2,1,0:T(8,128)(2,1)}) %reduce-scatter.5.cloned.1.call-update) | async-done | bytes 196624 | tf_op jit(solution)/shard_map/reduce_scatter | solution.py:85
  (141 shorter events, 106.1 us)
Async XLA Ops:
  7.2 78.0 %copy-start.6 = (bf16[8192,16]{0,1:T(8,128)(2,1)S(1)}, bf16[8192,16]{0,1:T(8,128)(2,1)}, u32[]{:S(2)}) copy-start(bf16[8192,16]{0,1:T(8,128)(2,1)} %param.26) | copy-start | bytes 786436
  7.2 78.7 %copy-start.7 = (bf16[512,18]{0,1:T(8,128)(2,1)S(1)}, bf16[512,18]{0,1:T(8,128)(2,1)}, u32[]{:S(2)}) copy-start(bf16[512,18]{0,1:T(8,128)(2,1)} %param.24) | copy-start | bytes 55300
  79.2 12.0 all-to-all-start.4
  91.2 74.2 %all-to-all-start.3 = ((bf16[16,512,16]{1,2,0:T(8,128)(2,1)}), bf16[16,512,16]{1,2,0:T(8,128)(2,1)S(1)}, u32[]{:S(2)}, u32[]{:S(2)}) async-start(bf16[16,512,16]{1,2,0:T(8,128)(2,1)} %bitcast.89), calls=%async_computation.3 | async-start | bytes 524288 | tf_op jit(solution)/shard_map/all_to_all | solution.py:154
  94.8 489.1 %all-gather.9.cloned.1.call-start = ((), (), s32[]{:S(2)}) async-start(), calls=%async_computation.14 | async-start | bytes 5048320 | tf_op jit(solution)/shard_map/all_gather | solution.py:46
  103.4 66.2 %copy-start.3 = (bf16[16,2,8192]{2,1,0:T(2,128)(2,1)S(1)}, bf16[16,2,8192]{2,1,0:T(2,128)(2,1)}, u32[]{:S(2)}) copy-start(bf16[16,2,8192]{2,1,0:T(2,128)(2,1)} %param.23) | copy-start | bytes 1572868
  169.5 426.5 %all-gather.7.cloned.1.call-start = ((), (), s32[]{:S(2)}) async-start(), calls=%async_computation.11 | async-start | bytes 8912896 | tf_op jit(solution)/shard_map/all_gather | solution.py:158
  208.7 24.2 %copy-start.11 = (bf16[4,32]{1,0:T(4,128)(2,1)S(1)}, bf16[4,32]{1,0:T(4,128)(2,1)}, u32[]{:S(2)}) copy-start(bf16[4,32]{1,0:T(4,128)(2,1)} %param.19) | copy-start | bytes 772
  208.7 24.2 %copy-start.13 = (bf16[2,32]{1,0:T(2,128)(2,1)S(1)}, bf16[2,32]{1,0:T(2,128)(2,1)}, u32[]{:S(2)}) copy-start(bf16[2,32]{1,0:T(2,128)(2,1)} %param.20) | copy-start | bytes 388
  208.7 24.2 %copy-start.5 = (bf16[2,4096]{1,0:T(2,128)(2,1)S(1)}, bf16[2,4096]{1,0:T(2,128)(2,1)}, u32[]{:S(2)}) copy-start(bf16[2,4096]{1,0:T(2,128)(2,1)} %param.15) | copy-start | bytes 49156
  212.8 363.0 %copy-start.4 = (bf16[3,32,512]{2,1,0:T(8,128)(2,1)S(1)}, bf16[3,32,512]{2,1,0:T(8,128)(2,1)}, u32[]{:S(2)}) copy-start(bf16[3,32,512]{2,1,0:T(8,128)(2,1)} %param.16) | copy-start | bytes 294916
  223.9 346.4 %all-to-all-start = ((bf16[256,2,16]{2,1,0:T(2,128)(2,1)}), bf16[256,2,16]{2,1,0:T(2,128)(2,1)S(1)}, u32[]{:S(2)}, u32[]{:S(2)}) async-start(bf16[256,2,16]{2,1,0:T(2,128)(2,1)} %stack.2), calls=%async_computation | async-start | bytes 262144 | tf_op jit(solution)/shard_map/all_to_all | solution.py:16
  572.2 11.5 all-to-all-start.1
  613.7 349.9 %copy-start.14 = (bf16[32]{0:T(256)(128)(2,1)S(1)}, bf16[32]{0:T(256)(128)(2,1)}, u32[]{:S(2)}) copy-start(bf16[32]{0:T(256)(128)(2,1)} %param.21) | copy-start | bytes 196
  613.8 449.7 %copy-start.8 = (s32[2,2]{1,0:T(2,128)S(1)}, s32[2,2]{1,0:T(2,128)}, u32[]{:S(2)}) copy-start(s32[2,2]{1,0:T(2,128)} %param.29) | copy-start | bytes 52
  614.8 465.0 %all-to-all-start.5 = ((bf16[16,32,288]{2,1,0:T(8,128)(2,1)}), bf16[16,32,288]{2,1,0:T(8,128)(2,1)S(1)}, u32[]{:S(2)}, u32[]{:S(2)}) async-start(bf16[16,32,288]{2,1,0:T(8,128)(2,1)} %broadcast_in_dim.25), calls=%async_computation.5 | async-start | bytes 786432 | tf_op jit(solution)/shard_map/all_to_all | solution.py:28
  1086.0 371.4 %all-to-all-start.6 = ((bf16[16,2,4096]{2,1,0:T(2,128)(2,1)}), bf16[16,2,4096]{2,1,0:T(2,128)(2,1)S(1)}, u32[]{:S(2)}, u32[]{:S(2)}) async-start(bf16[16,2,4096]{2,1,0:T(2,128)(2,1)} %reshape.268), calls=%async_computation.6 | async-start | bytes 524288 | tf_op jit(solution)/shard_map/all_to_all | solution.py:65
  1111.7 17.7 %copy-start.10 = (bf16[16,16]{1,0:T(8,128)(2,1)S(1)}, bf16[16,16]{1,0:T(8,128)(2,1)}, u32[]{:S(2)}) copy-start(bf16[16,16]{1,0:T(8,128)(2,1)} %param.27) | copy-start | bytes 1540
  1457.4 39.4 %all-to-all-start.8 = ((bf16[16,2,24576]{2,1,0:T(2,128)(2,1)}), bf16[16,2,24576]{2,1,0:T(2,128)(2,1)S(1)}, u32[]{:S(2)}, u32[]{:S(2)}) async-start(bf16[16,2,24576]{2,1,0:T(2,128)(2,1)} %reshape.312), calls=%async_computation.8 | async-start | bytes 3145728 | tf_op jit(solution)/shard_map/all_to_all | solution.py:145
  1495.9 38.2 %copy-start = (bf16[64,4097]{1,0:T(8,128)(2,1)}, bf16[64,4097]{1,0:T(8,128)(2,1)S(1)}, u32[]{:S(2)}) copy-start(bf16[64,4097]{1,0:T(8,128)(2,1)S(1)} %reshape.284) | copy-start | bytes 1573252
  1496.9 63.7 %all-to-all-start.7 = ((bf16[64,16,256]{2,0,1:T(8,128)(2,1)}), bf16[64,16,256]{2,0,1:T(8,128)(2,1)S(1)}, u32[]{:S(2)}, u32[]{:S(2)}) async-start(bf16[64,16,256]{2,0,1:T(8,128)(2,1)} %bitcast.88), calls=%async_computation.7 | async-start | bytes 1048576 | tf_op jit(solution)/shard_map/all_to_all | solution.py:232
  1521.9 89.4 %reduce-scatter.3.cloned.1.call-start = ((), (), s32[]{:S(2)}) async-start(), calls=%async_computation.12 | async-start | bytes 3932160 | tf_op jit(solution)/shard_map/reduce_scatter | solution.py:85
  1568.4 43.0 %slice-start.1 = ((bf16[3,32,512]{2,1,0:T(8,128)(2,1)}), bf16[2,32,512]{2,1,0:T(8,128)(2,1)S(1)}, s32[]{:S(2)}) async-start(bf16[3,32,512]{2,1,0:T(8,128)(2,1)} %param.16), calls=%async_computation.16 | async-start | bytes 131072 | tf_op jit(solution)/shard_map/slice | solution.py:177
  1572.3 73.2 %reduce-scatter.5.cloned.1.call-start = ((), (), s32[]{:S(2)}) async-start(), calls=%async_computation.13 | async-start | bytes 983040 | tf_op jit(solution)/shard_map/reduce_scatter | solution.py:85
  (5 other events, 47.9 us)
Sparse Core Ops, SparseCore 0:
  169.6 88.0 all-gather.8
  260.7 115.8 all-gather.6
  1572.4 38.8 reduce-scatter.2
  1613.7 31.7 reduce-scatter.4
